TPU v7x, 32 devices: a whole 2x2x4 slice. The times are simulated.
32 devices in a mesh: energy: 8 (over z, x), slab: 4 (over y, core).
Axes of the slice: x: 2, y: 2, z: 4, core: 2. Of those that a mesh axis runs over, the one named last changes fastest.
Arguments:
- green_blocks: bfloat16 [8, 4, 512, 512], P('energy', 'slab'), may hold values from -6 to 6
- coulomb: bfloat16 [4, 512, 512], P('slab'), may hold values from -0.25 to 0.25
- couple_cols: int32 [4, 128, 8], P('slab'), may hold values from 0 to 127
- couple_vals: bfloat16 [4, 128, 8], P('slab'), may hold values from -0.8984375 to 0.8984375
Outputs:
- new_green: bfloat16 [8, 4, 512, 512], P('energy', 'slab')
Inputs may be any that keep to these rules, and one draw needn't show every extreme that they name: couple_cols[s, i, k] names one of the first 128 orbitals of slab s + 1.
All inputs are finite; a program needn't handle non-finite values.
Results may differ from a plain program's by a relative error of at most 0.015.
Values may be sent and summed in bfloat16 or wider, within the bound.
A program may use at most 64 MiB of HBM per device.

v0:
```python
import math

import jax
import jax.numpy as jnp
from jax import lax
from jax.sharding import PartitionSpec as P


def from_behind(x, axis, by):
    size = lax.axis_size(axis)
    pairs = [(i, i + by) for i in range(size) if 0 <= i + by < size]
    return lax.ppermute(x, axis, pairs)


def plain_dot(left, right):
    return jnp.dot(left, right, preferred_element_type=jnp.float32)


def split_parts(values):
    upper = values.astype(jnp.bfloat16)
    lower = (values - upper.astype(jnp.float32)).astype(jnp.bfloat16)
    return (upper, lower)


def coupling_matrix(column_ids, coupling_values):
    width = column_ids.shape[0]
    hits = column_ids[:, :, None] == jnp.arange(width, dtype=jnp.int32)[None, None, :]
    summed = jnp.sum(
        jnp.where(hits, coupling_values.astype(jnp.float32)[:, :, None], jnp.float32(0.0)), axis=1
    )
    return summed.astype(jnp.bfloat16)


def on_device(green_blocks, coulomb, couple_cols, couple_vals):
    own_green = green_blocks[:, 0]
    coulomb_block = coulomb[0]
    per_device = own_green.shape[0]
    orbitals = own_green.shape[1]
    volume = lax.axis_size("energy")
    energies = per_device * volume
    inv_root = 1.0 / math.sqrt(orbitals)
    flipped = jnp.swapaxes(own_green, 1, 2)
    received, flipped_recv = (
        lax.all_to_all(own_green, "energy", split_axis=1, concat_axis=0, tiled=True),
        lax.all_to_all(flipped, "energy", split_axis=1, concat_axis=0, tiled=True),
    )
    green_entries = received.reshape(energies, -1)
    flipped_entries = flipped_recv.reshape(energies, -1)
    entry_shape = received.shape
    halfway = energies // 2 + 1
    frequency = jnp.arange(halfway, dtype=jnp.int32)
    energy_index = jnp.arange(energies, dtype=jnp.int32)
    angles = (frequency[:, None] * energy_index[None, :] % energies).astype(jnp.float32) * (
        2.0 * math.pi / energies
    )
    cosine = jnp.cos(angles)
    sine = jnp.sin(angles)
    weights = (
        jnp.where((frequency == 0) | (2 * frequency == energies), 1.0, 2.0).astype(jnp.float32)
        / energies
    )
    forward_high, forward_low = split_parts(jnp.concatenate([cosine, -sine], axis=0))
    backward_table = jnp.concatenate(
        [cosine * weights[:, None], -sine * weights[:, None]], axis=0
    ).T
    backward_high, backward_low = split_parts(backward_table)

    def spectrum(entries):
        stacked = plain_dot(forward_high, entries) + plain_dot(forward_low, entries)
        return (stacked[:halfway], stacked[halfway:])

    def to_values(real_part, imag_part):
        data_high, data_low = split_parts(jnp.concatenate([real_part, imag_part], axis=0))
        return (
            plain_dot(backward_high, data_high)
            + plain_dot(backward_high, data_low)
            + plain_dot(backward_low, data_high)
        )

    green_real, green_imag = spectrum(green_entries)
    mirror_real, mirror_imag = spectrum(flipped_entries)
    polar_entries = to_values(
        green_real * mirror_real + green_imag * mirror_imag,
        green_imag * mirror_real - green_real * mirror_imag,
    )
    polar_entries = (polar_entries * (0.5 / math.sqrt(orbitals * energies))).astype(jnp.bfloat16)
    polar = lax.all_to_all(
        polar_entries.reshape(entry_shape), "energy", split_axis=0, concat_axis=1, tiled=True
    )
    inner = jnp.einsum(
        "ij,ejk->eik", coulomb_block, polar, preferred_element_type=jnp.float32
    ).astype(jnp.bfloat16)
    second = jnp.einsum("eij,jk->eik", inner, coulomb_block, preferred_element_type=jnp.float32)
    third = jnp.einsum(
        "eij,ejk->eik", inner, second.astype(jnp.bfloat16), preferred_element_type=jnp.float32
    )
    screened = (coulomb_block.astype(jnp.float32)[None] + second + third).astype(jnp.bfloat16)
    screened_entries = lax.all_to_all(
        screened, "energy", split_axis=1, concat_axis=0, tiled=True
    ).reshape(energies, -1)
    screen_real, screen_imag = spectrum(screened_entries)
    sigma_entries = to_values(
        green_real * screen_real - green_imag * screen_imag,
        green_real * screen_imag + green_imag * screen_real,
    )
    sigma_entries = (sigma_entries * (0.2 / math.sqrt(energies))).astype(jnp.bfloat16)
    sigma = lax.all_to_all(
        sigma_entries.reshape(entry_shape), "energy", split_axis=0, concat_axis=1, tiled=True
    )
    interface = couple_cols.shape[1]
    last = orbitals - interface
    coupling = coupling_matrix(couple_cols[0], couple_vals[0])
    prev_green, previous = from_behind((own_green, coupling), "slab", 1)
    next_green = from_behind(own_green, "slab", -1)
    prev_corner = prev_green[:, last:, last:]
    next_corner = next_green[:, :interface, :interface]
    near_next = jnp.einsum(
        "ij,ejk->eik", coupling, next_corner, preferred_element_type=jnp.float32
    ).astype(jnp.bfloat16)
    near_prev = jnp.einsum(
        "ji,ejk->eik", previous, prev_corner, preferred_element_type=jnp.float32
    ).astype(jnp.bfloat16)
    right_part = (
        jnp.einsum("eij,kj->eik", near_next, coupling, preferred_element_type=jnp.float32)
        * inv_root
    )
    left_part = (
        jnp.einsum("eij,jk->eik", near_prev, previous, preferred_element_type=jnp.float32)
        * inv_root
    )
    total = sigma.astype(jnp.float32)
    total = total.at[:, last:, last:].add(right_part)
    total = total.at[:, :interface, :interface].add(left_part)
    total_b = total.astype(jnp.bfloat16)
    dressed = jnp.einsum(
        "eij,ejk->eik", own_green, total_b, preferred_element_type=jnp.float32
    ).astype(jnp.bfloat16)
    updated = (
        own_green
        + jnp.einsum("eij,ejk->eik", dressed, own_green, preferred_element_type=jnp.float32)
        * inv_root
    )
    return updated.astype(jnp.bfloat16)[:, None]


def solution(mesh):
    return jax.shard_map(
        on_device,
        mesh=mesh,
        in_specs=(
            P("energy", "slab", None, None),
            P("slab", None, None),
            P("slab", None, None),
            P("slab", None, None),
        ),
        out_specs=P("energy", "slab", None, None),
        check_vma=False,
    )
```

profile of v0, /device:TPU:0, one launch (start us, length us, event | category | flops | bytes accessed | tf_op | source)
XLA Modules:
  0.0 132.9 jit_solution(15533426372534558874)
XLA Ops:
  0.0 1.9 %copy.36 = bf16[1,512,512]{2,0,1:T(2,128)(2,1)S(1)} copy(bf16[1,512,512]{2,1,0:T(8,128)(2,1)} %bitcast.105) | data formatting | bytes 1048576 | tf_op jit(solution)/shard_map/squeeze | solution.py:35
  1.9 0.6 broadcast.121
  2.5 3.9 %reduce.11 = bf16[512,512]{1,0:T(8,128)(2,1)S(1)} reduce(bf16[512,1,512]{2,1,0:T(2,128)(2,1)S(1)} %bitcast.102, bf16[]{:T(256)} %broadcast.121), dimensions={1}, to_apply=%bitcast.100.reduce_sub_computation | reduce | bytes 1048578
  6.3 1.2 reshape.211
  7.5 7.3 %all-to-all-start = ((bf16[8,2,16384]{2,1,0:T(2,128)(2,1)}), bf16[8,2,16384]{2,1,0:T(2,128)(2,1)S(1)}, u32[]{:S(2)}, u32[]{:S(2)}) async-start(bf16[8,2,16384]{2,1,0:T(2,128)(2,1)} %reshape.211), calls=%async_computation | async-start | bytes 1048576 | tf_op jit(solution)/shard_map/all_to_all | solution.py:44
  14.8 0.9 copy.27
  15.7 3.9 %reduce.10 = bf16[512,512]{1,0:T(8,128)(2,1)S(1)} reduce(bf16[512,1,512]{2,1,0:T(2,128)(2,1)S(1)} %bitcast.104, bf16[]{:T(256)} %broadcast.121), dimensions={1}, to_apply=%bitcast.75.reduce_sub_computation | reduce | bytes 1048578
  19.6 1.2 reshape.209
  20.8 8.5 %all-to-all-done = bf16[8,2,16384]{2,1,0:T(2,128)(2,1)S(1)} async-done(((bf16[8,2,16384]{2,1,0:T(2,128)(2,1)}), bf16[8,2,16384]{2,1,0:T(2,128)(2,1)S(1)}, u32[]{:S(2)}, u32[]{:S(2)}) %all-to-all-start) | async-done | bytes 524320 | tf_op jit(solution)/shard_map/all_to_all | solution.py:44
  29.3 4.3 %all-to-all-start.1 = ((bf16[8,2,16384]{2,1,0:T(2,128)(2,1)}), bf16[8,2,16384]{2,1,0:T(2,128)(2,1)}, u32[]{:S(2)}, u32[]{:S(2)}) async-start(bf16[8,2,16384]{2,1,0:T(2,128)(2,1)} %reshape.209), calls=%async_computation.1 | async-start | bytes 1048576 | tf_op jit(solution)/shard_map/all_to_all | solution.py:45
  33.7 0.5 reshape.212
  34.2 3.1 %bitcast_reduce_fusion.1 = bf16[512,512]{1,0:T(8,128)(2,1)S(1)} fusion(bf16[512,1,512]{2,1,0:T(2,128)(2,1)S(1)} %reshape.212), kind=kLoop, calls=%fused_computation.88 | loop fusion | bytes 1048576 | tf_op jit(solution)/shard_map/all_to_all | solution.py:44
  38.4 9.3 %all-to-all-done.1 = bf16[8,2,16384]{2,1,0:T(2,128)(2,1)} async-done(((bf16[8,2,16384]{2,1,0:T(2,128)(2,1)}), bf16[8,2,16384]{2,1,0:T(2,128)(2,1)}, u32[]{:S(2)}, u32[]{:S(2)}) %all-to-all-start.1) | async-done | bytes 524320 | tf_op jit(solution)/shard_map/all_to_all | solution.py:45
  47.7 2.2 %reshape.210 = bf16[512,1,512]{2,1,0:T(2,128)(2,1)S(1)} reshape(bf16[8,2,16384]{2,1,0:T(2,128)(2,1)} %all-to-all-done.1) | data formatting | bytes 1048576
  49.9 3.9 %bitcast_reduce_fusion.2 = bf16[512,512]{1,0:T(8,128)(2,1)} fusion(bf16[512,1,512]{2,1,0:T(2,128)(2,1)S(1)} %reshape.210), kind=kLoop, calls=%fused_computation.89 | loop fusion | bytes 1048576 | tf_op jit(solution)/shard_map/all_to_all | solution.py:45
  53.8 1.3 reshape.193
  56.7 0.5 convolution_add_fusion.6
  57.8 18.0 %all_to_all.20 = bf16[8,64,512]{2,1,0:T(8,128)(2,1)S(1)} all-to-all(bf16[8,64,512]{2,1,0:T(8,128)(2,1)S(1)} %copy.28), channel_id=1, replica_groups=mesh['energy'=8,'slab'=4] {'energy'}, dimensions={0} | all-to-all | bytes 1048576 | tf_op jit(solution)/shard_map/all_to_all | solution.py:87
  77.3 0.8 copy.35
  78.1 4.7 %reduce.12 = bf16[512,512]{1,0:T(8,128)(2,1)} reduce(bf16[512,1,512]{2,1,0:T(2,128)(2,1)S(1)} %bitcast.103, bf16[]{:T(256)} %broadcast.121), dimensions={1}, to_apply=%bitcast.99.reduce_sub_computation | reduce | bytes 1048578
  82.7 1.4 %reshape.213 = bf16[8,2,16384]{2,1,0:T(2,128)(2,1)S(1)} reshape(bf16[512,512]{1,0:T(8,128)(2,1)} %reduce.12) | data formatting | bytes 1048576
  84.2 17.6 %all_to_all.21 = bf16[8,2,16384]{2,1,0:T(2,128)(2,1)} all-to-all(bf16[8,2,16384]{2,1,0:T(2,128)(2,1)S(1)} %reshape.213), channel_id=1, replica_groups=mesh['energy'=8,'slab'=4] {'energy'}, dimensions={0} | all-to-all | bytes 1048576 | tf_op jit(solution)/shard_map/all_to_all | solution.py:98
  101.8 2.2 %reshape.214 = bf16[512,1,512]{2,1,0:T(2,128)(2,1)S(1)} reshape(bf16[8,2,16384]{2,1,0:T(2,128)(2,1)} %all_to_all.21) | data formatting | bytes 1048576
  104.0 3.9 %bitcast_reduce_fusion = bf16[512,512]{1,0:T(8,128)(2,1)} fusion(bf16[512,1,512]{2,1,0:T(2,128)(2,1)S(1)} %reshape.214), kind=kLoop, calls=%fused_computation.87 | loop fusion | bytes 1048576 | tf_op jit(solution)/shard_map/all_to_all | solution.py:98
  107.9 1.3 reshape.197
  111.8 0.9 copy.30
  112.7 3.6 %all-to-all-start.4 = ((bf16[8,64,512]{2,1,0:T(8,128)(2,1)}), bf16[8,64,512]{2,1,0:T(8,128)(2,1)S(1)}, u32[]{:S(2)}, u32[]{:S(2)}) async-start(bf16[8,64,512]{2,1,0:T(8,128)(2,1)} %copy.30), calls=%async_computation.4 | async-start | bytes 1048576 | tf_op jit(solution)/shard_map/all_to_all | solution.py:107
  116.4 1.3 collective-permute-start
  117.7 3.1 %collective-permute-start.2 = (bf16[1,512,512]{2,1,0:T(8,128)(2,1)S(1)}, bf16[1,512,512]{2,1,0:T(8,128)(2,1)S(1)}, u32[]{:S(2)}, u32[]{:S(2)}) collective-permute-start(bf16[1,512,512]{2,1,0:T(8,128)(2,1)S(1)} %bitcast.108), channel_id=1, source_target_pairs={{0,1},{1,2},{2,3},{4,5},{5,6},{6,7},{8,9},{9,10},{10,11},{12,13},{... | collective-permute-start | bytes 1572872 | tf_op jit(solution)/shard_map/ppermute | solution.py:12
  121.3 3.0 %collective-permute-start.1 = (bf16[128,128]{1,0:T(8,128)(2,1)S(1)}, bf16[128,128]{1,0:T(8,128)(2,1)S(1)}, u32[]{:S(2)}, u32[]{:S(2)}) collective-permute-start(bf16[128,128]{1,0:T(8,128)(2,1)S(1)} %select_reduce_fusion), channel_id=1, source_target_pairs={{0,1},{1,2},{2,3},{4,5},{5,6},{6,7},{8,9},{9,10},{10,11},{12,13},{... | collective-permute-start | bytes 98312 | tf_op jit(solution)/shard_map/ppermute | solution.py:12
  124.3 6.1 %all-to-all-done.4 = bf16[8,64,512]{2,1,0:T(8,128)(2,1)S(1)} async-done(((bf16[8,64,512]{2,1,0:T(8,128)(2,1)}), bf16[8,64,512]{2,1,0:T(8,128)(2,1)S(1)}, u32[]{:S(2)}, u32[]{:S(2)}) %all-to-all-start.4) | async-done | bytes 524320 | tf_op jit(solution)/shard_map/all_to_all | solution.py:107
  131.2 1.6 %fusion.10 = bf16[1,1,512,512]{3,2,1,0:T(8,128)(2,1)} fusion(bf16[1,1,512,512]{3,2,1,0:T(8,128)(2,1)S(1)} %copy-done.2, f32[1,512,512]{2,1,0:T(8,128)S(1)} %fusion.17), kind=kOutput, calls=%fused_computation.25 | convolution fusion | flops 538443776 | bytes 2097152 | tf_op jit(solution)/shard_map/eij,ejk->eik/dot_general | solution.py:140
  (41 shorter events, 8.7 us)
Async XLA Ops:
  1.9 12.9 %copy-start.1 = (bf16[1,1,512,512]{3,2,1,0:T(8,128)(2,1)S(1)}, bf16[1,1,512,512]{3,2,1,0:T(8,128)(2,1)}, u32[]{:S(2)}) copy-start(bf16[1,1,512,512]{3,2,1,0:T(8,128)(2,1)} %param.8) | copy-start | bytes 1572868
  7.5 21.8 %all-to-all-start = ((bf16[8,2,16384]{2,1,0:T(2,128)(2,1)}), bf16[8,2,16384]{2,1,0:T(2,128)(2,1)S(1)}, u32[]{:S(2)}, u32[]{:S(2)}) async-start(bf16[8,2,16384]{2,1,0:T(2,128)(2,1)} %reshape.211), calls=%async_computation | async-start | bytes 1048576 | tf_op jit(solution)/shard_map/all_to_all | solution.py:44
  29.3 18.4 %all-to-all-start.1 = ((bf16[8,2,16384]{2,1,0:T(2,128)(2,1)}), bf16[8,2,16384]{2,1,0:T(2,128)(2,1)}, u32[]{:S(2)}, u32[]{:S(2)}) async-start(bf16[8,2,16384]{2,1,0:T(2,128)(2,1)} %reshape.209), calls=%async_computation.1 | async-start | bytes 1048576 | tf_op jit(solution)/shard_map/all_to_all | solution.py:45
  57.2 18.6 %copy-start = (bf16[1,512,512]{2,1,0:T(8,128)(2,1)S(1)}, bf16[1,512,512]{2,1,0:T(8,128)(2,1)}, u32[]{:S(2)}) copy-start(bf16[1,512,512]{2,1,0:T(8,128)(2,1)} %param.9) | copy-start | bytes 1572868
  111.3 5.1 %copy-start.2 = (bf16[1,1,512,512]{3,2,1,0:T(8,128)(2,1)S(1)}, bf16[1,1,512,512]{3,2,1,0:T(8,128)(2,1)}, u32[]{:S(2)}) copy-start(bf16[1,1,512,512]{3,2,1,0:T(8,128)(2,1)} %param.8) | copy-start | bytes 1572868
  111.3 9.4 %copy-start.4 = (bf16[1,128,8]{1,2,0:T(8,128)(2,1)S(1)}, bf16[1,128,8]{1,2,0:T(8,128)(2,1)}, u32[]{:S(2)}) copy-start(bf16[1,128,8]{1,2,0:T(8,128)(2,1)} %param.11) | copy-start | bytes 6148
  111.3 9.5 %copy-start.3 = (s32[1,128,8]{1,2,0:T(8,128)S(1)}, s32[1,128,8]{1,2,0:T(8,128)}, u32[]{:S(2)}) copy-start(s32[1,128,8]{1,2,0:T(8,128)} %param.10) | copy-start | bytes 12292
  112.7 17.7 %all-to-all-start.4 = ((bf16[8,64,512]{2,1,0:T(8,128)(2,1)}), bf16[8,64,512]{2,1,0:T(8,128)(2,1)S(1)}, u32[]{:S(2)}, u32[]{:S(2)}) async-start(bf16[8,64,512]{2,1,0:T(8,128)(2,1)} %copy.30), calls=%async_computation.4 | async-start | bytes 1048576 | tf_op jit(solution)/shard_map/all_to_all | solution.py:107
  116.4 14.2 %collective-permute-start = (bf16[1,512,512]{2,1,0:T(8,128)(2,1)S(1)}, bf16[1,512,512]{2,1,0:T(8,128)(2,1)S(1)}, u32[]{:S(2)}, u32[]{:S(2)}) collective-permute-start(bf16[1,512,512]{2,1,0:T(8,128)(2,1)S(1)} %bitcast.107), channel_id=1, source_target_pairs={{1,0},{2,1},{3,2},{5,4},{6,5},{7,6},{9,8},{10,9},{11,10},{13,12},{... | collective-permute-start | bytes 1572872 | tf_op jit(solution)/shard_map/ppermute | solution.py:12
  117.7 13.2 %collective-permute-start.2 = (bf16[1,512,512]{2,1,0:T(8,128)(2,1)S(1)}, bf16[1,512,512]{2,1,0:T(8,128)(2,1)S(1)}, u32[]{:S(2)}, u32[]{:S(2)}) collective-permute-start(bf16[1,512,512]{2,1,0:T(8,128)(2,1)S(1)} %bitcast.108), channel_id=1, source_target_pairs={{0,1},{1,2},{2,3},{4,5},{5,6},{6,7},{8,9},{9,10},{10,11},{12,13},{... | collective-permute-start | bytes 1572872 | tf_op jit(solution)/shard_map/ppermute | solution.py:12
  121.3 9.6 %collective-permute-start.1 = (bf16[128,128]{1,0:T(8,128)(2,1)S(1)}, bf16[128,128]{1,0:T(8,128)(2,1)S(1)}, u32[]{:S(2)}, u32[]{:S(2)}) collective-permute-start(bf16[128,128]{1,0:T(8,128)(2,1)S(1)} %select_reduce_fusion), channel_id=1, source_target_pairs={{0,1},{1,2},{2,3},{4,5},{5,6},{6,7},{8,9},{9,10},{10,11},{12,13},{... | collective-permute-start | bytes 98312 | tf_op jit(solution)/shard_map/ppermute | solution.py:12
where the time goes:
time: 134 us; the launch traced here: 133 us
  blocking collectives  35.7 us (27%)
  local copies, waits for them, and re-layouts  27.8 us (21%)
  waiting for transfers between devices  23.9 us (18%)
  starting transfers between devices  22.6 us (17%)
  other arithmetic  13.7 us (10%)
  matrix products  8.85 us (7%)
    all_to_all x1, blocking collectives, on_device(): lax.all_to_all(polar_entries.reshape(entry_shape), 'energy', split_axis=0...  18 us
    all_to_all x1, blocking collectives, on_device(): lax.all_to_all(screened, 'energy', split_axis=1, concat_axis=0, tiled=True)  17.6 us
    unnamed x3, other arithmetic  12.4 us
    unnamed x17, local copies, waits for them, and re-layouts  9.36 us
    all_to_all x1, waiting for transfers between devices, on_device(): lax.all_to_all(flipped, 'energy', split_axis=1, concat_axis=0, tiled=True)  9.3 us
    all_to_all x1, waiting for transfers between devices, on_device(): lax.all_to_all(own_green, 'energy', split_axis=1, concat_axis=0, tiled=True)  8.47 us
    ppermute x3, starting transfers between devices, from_behind(): return lax.ppermute(x, axis, pairs)  7.36 us
    all_to_all x1, starting transfers between devices, on_device(): lax.all_to_all(own_green, 'energy', split_axis=1, concat_axis=0, tiled=True)  7.28 us
  transfers between devices with their start and end apart: 6, of which 3 were waited for; matrix products, arithmetic and copies ran while one was open for 9% of the time, Pallas kernels for 0%

commit v1 on v0

--- a/solution.py
+++ b/solution.py
@@ -1,8 +1,11 @@
+import functools
 import math
 
 import jax
 import jax.numpy as jnp
 from jax import lax
+from jax.experimental import pallas as pl
+from jax.experimental.pallas import tpu as pltpu
 from jax.sharding import PartitionSpec as P
 
 
@@ -143,9 +146,277 @@
     return updated.astype(jnp.bfloat16)[:, None]
 
 
+MESH = pl.DeviceIdType.MESH
+
+
+def unit_blocks(unit, grid):
+    odd = grid - 1
+    paired = grid * odd // 2
+    slot = unit // odd
+    turn = unit % odd
+    diagonal = unit // paired
+    first = (turn + slot) % odd
+    second = (turn + odd - slot) % odd
+    lone = 1 - (slot + odd - 1) // odd
+    row = lone * odd + (1 - lone) * first
+    col = lone * turn + (1 - lone) * second
+    corner = 2 * (unit - paired)
+    row0 = diagonal * corner + (1 - diagonal) * row
+    col0 = diagonal * corner + (1 - diagonal) * col
+    row1 = diagonal * (corner + 1) + (1 - diagonal) * col
+    col1 = diagonal * (corner + 1) + (1 - diagonal) * row
+    return ((row0, col0), (row1, col1))
+
+
+def fused_kernel(
+    volume, slabs, grid, scale_polar, scale_sigma, inv_root,
+    green, coulomb, cols, vals, out,
+    green_in, mirror, polar_out, polar_in, matrix, inner, screened, screen_in, sigma_out, sigma_in,
+    coupling, turned, next_corner, left_out, left_in, total,
+    send_sem, recv_sem, slab_send, slab_recv,
+):
+    me = lax.axis_index("energy")
+    slab = lax.axis_index("slab")
+    size = green.shape[0] // grid
+    last = green.shape[0] - size
+    order = sorted(range(1, volume), key=lambda k: (-min(k, volume - k), k))
+    has_prev = 1 - (slabs - 1 - slab + 0) // (slabs - 1)
+    has_next = 1 - slab // (slabs - 1)
+    diagonal = me // (grid * (grid - 1) // 2)
+
+    def peer_of(k):
+        return lax.rem(me + k, volume)
+
+    barrier = pltpu.get_barrier_semaphore()
+    for k in range(1, volume):
+        pl.semaphore_signal(barrier, inc=1, device_id=(peer_of(k), slab), device_id_type=MESH)
+
+    @pl.when(slab > 0)
+    def _():
+        pl.semaphore_signal(barrier, inc=1, device_id=(me, slab - 1), device_id_type=MESH)
+
+    @pl.when(slab < slabs - 1)
+    def _():
+        pl.semaphore_signal(barrier, inc=1, device_id=(me, slab + 1), device_id_type=MESH)
+
+    pl.semaphore_wait(barrier, volume - 1 + has_prev + has_next)
+
+    def block_of(ref, coords):
+        row = pl.multiple_of(coords[0] * size, size)
+        col = pl.multiple_of(coords[1] * size, size)
+        return ref.at[pl.ds(row, size), pl.ds(col, size)]
+
+    def remote(src, dst, phase, k, half):
+        return pltpu.make_async_remote_copy(
+            src_ref=src, dst_ref=dst,
+            send_sem=send_sem.at[phase, k, half], recv_sem=recv_sem.at[phase, k, half],
+            device_id=(peer_of(k), slab), device_id_type=MESH,
+        )
+
+    def scatter(source, landing, phase):
+        copies = []
+        for k in order:
+            coords = unit_blocks(peer_of(k), grid)
+            for half in range(2):
+                copy = remote(block_of(source, coords[half]), landing.at[me, half], phase, k, half)
+                copy.start()
+                copies.append(copy)
+        own = unit_blocks(me, grid)
+        for half in range(2):
+            landing[me, half] = block_of(source, own[half])[...]
+        return copies
+
+    def gather(source, landing, phase, half):
+        copies = []
+        for k in order:
+            copy = remote(source.at[peer_of(k), half], landing.at[me, half], phase, k, half)
+            copy.start()
+            copies.append(copy)
+        landing[me, half] = source[me, half]
+        return copies
+
+    def arrived(copies):
+        for copy in copies:
+            copy.wait_recv()
+
+    def assemble(landing, target):
+        for unit in range(volume):
+            coords = unit_blocks(unit, grid)
+            for half in range(2):
+                row, col = coords[half]
+                target[row * size:(row + 1) * size, col * size:(col + 1) * size] = landing[unit, half]
+
+    sent = scatter(green, green_in, 0)
+    corner_copy = pltpu.make_async_remote_copy(
+        src_ref=green.at[pl.ds(0, size), pl.ds(0, size)], dst_ref=next_corner,
+        send_sem=slab_send.at[0], recv_sem=slab_recv.at[0],
+        device_id=(me, slab - has_prev), device_id_type=MESH,
+    )
+    left_copy = pltpu.make_async_remote_copy(
+        src_ref=left_out, dst_ref=left_in,
+        send_sem=slab_send.at[1], recv_sem=slab_recv.at[1],
+        device_id=(me, slab + has_next), device_id_type=MESH,
+    )
+
+    @pl.when(slab > 0)
+    def _():
+        corner_copy.start()
+
+    ids = cols[...]
+    values = vals[...].astype(jnp.float32)
+    columns = lax.broadcasted_iota(jnp.int32, (size, size), 1)
+    summed = jnp.zeros((size, size), jnp.float32)
+    for k in range(ids.shape[1]):
+        summed += jnp.where(ids[:, k:k + 1] == columns, values[:, k:k + 1], jnp.float32(0.0))
+    summed = summed.astype(jnp.bfloat16).astype(jnp.float32)
+    coupling[...] = summed.astype(jnp.bfloat16)
+    turned[...] = summed.T.astype(jnp.bfloat16)
+
+    @pl.when(slab < slabs - 1)
+    def _():
+        near_prev = plain_dot(turned[...], green[last:, last:]).astype(jnp.bfloat16)
+        left_out[...] = plain_dot(near_prev, coupling[...]) * inv_root
+        left_copy.start()
+
+    arrived(sent)
+    everything = list(sent)
+    rows_at_once = 16
+
+    for half in range(2):
+        other = diagonal * half + (1 - diagonal) * (1 - half)
+
+        def flip(e, carry, half=half, other=other):
+            mirror[e, half] = green_in[e, other].astype(jnp.float32).T
+            return carry
+
+        lax.fori_loop(0, volume, flip, 0)
+
+    for half in range(2):
+        def correlate(step, carry, half=half):
+            rows = pl.ds(pl.multiple_of(step * rows_at_once, rows_at_once), rows_at_once)
+            mine = [green_in[e, half, rows, :].astype(jnp.float32) for e in range(volume)]
+            theirs = [mirror[e, half, rows, :] for e in range(volume)]
+            for e in range(volume):
+                acc = mine[0] * theirs[(0 - e) % volume]
+                for e2 in range(1, volume):
+                    acc += mine[e2] * theirs[(e2 - e) % volume]
+                polar_out[e, half, rows, :] = (acc * scale_polar).astype(jnp.bfloat16)
+            return carry
+
+        lax.fori_loop(0, size // rows_at_once, correlate, 0)
+        copies = gather(polar_out, polar_in, 1, half)
+        everything += copies
+        if half == 0:
+            polar_copies = copies
+        else:
+            polar_copies = polar_copies + copies
+    arrived(polar_copies)
+    assemble(polar_in, matrix)
+    inner[...] = plain_dot(coulomb[...], matrix[...]).astype(jnp.bfloat16)
+    second = plain_dot(inner[...], coulomb[...])
+    total[...] = second
+    matrix[...] = second.astype(jnp.bfloat16)
+    third = plain_dot(inner[...], matrix[...])
+    screened[...] = (coulomb[...].astype(jnp.float32) + total[...] + third).astype(jnp.bfloat16)
+    copies = scatter(screened, screen_in, 2)
+    everything += copies
+    arrived(copies)
+
+    sigma_copies = []
+    for half in range(2):
+        def convolve(step, carry, half=half):
+            rows = pl.ds(pl.multiple_of(step * rows_at_once, rows_at_once), rows_at_once)
+            mine = [green_in[e, half, rows, :].astype(jnp.float32) for e in range(volume)]
+            waves = [screen_in[e, half, rows, :].astype(jnp.float32) for e in range(volume)]
+            for e in range(volume):
+                acc = mine[0] * waves[e]
+                for e2 in range(1, volume):
+                    acc += mine[e2] * waves[(e - e2) % volume]
+                sigma_out[e, half, rows, :] = (acc * scale_sigma).astype(jnp.bfloat16)
+            return carry
+
+        lax.fori_loop(0, size // rows_at_once, convolve, 0)
+        sigma_copies += gather(sigma_out, sigma_in, 3, half)
+    everything += sigma_copies
+    arrived(sigma_copies)
+    assemble(sigma_in, matrix)
+
+    @pl.when(slab < slabs - 1)
+    def _():
+        corner_copy.wait_recv()
+        near_next = plain_dot(coupling[...], next_corner[...]).astype(jnp.bfloat16)
+        right_part = plain_dot(near_next, turned[...]) * inv_root
+        matrix[last:, last:] = (matrix[last:, last:].astype(jnp.float32) + right_part).astype(jnp.bfloat16)
+        left_copy.wait_send()
+
+    @pl.when(slab > 0)
+    def _():
+        left_copy.wait_recv()
+        matrix[:size, :size] = (matrix[:size, :size].astype(jnp.float32) + left_in[...]).astype(jnp.bfloat16)
+        corner_copy.wait_send()
+
+    inner[...] = plain_dot(green[...], matrix[...]).astype(jnp.bfloat16)
+    updated = green[...].astype(jnp.float32) + plain_dot(inner[...], green[...]) * inv_root
+    out[...] = updated.astype(jnp.bfloat16)
+    for copy in everything:
+        copy.wait_send()
+
+
+def fused_on_device(grid, green_blocks, coulomb, couple_cols, couple_vals):
+    volume = lax.axis_size("energy")
+    slabs = lax.axis_size("slab")
+    orbitals = green_blocks.shape[-1]
+    size = orbitals // grid
+    half_type = jnp.bfloat16
+    pieces = pltpu.VMEM((volume, 2, size, size), half_type)
+    whole = pltpu.VMEM((orbitals, orbitals), half_type)
+    block = pltpu.VMEM((size, size), half_type)
+    wide = pltpu.VMEM((size, size), jnp.float32)
+    result = pl.pallas_call(
+        functools.partial(
+            fused_kernel, volume, slabs, grid,
+            0.5 / math.sqrt(orbitals * volume), 0.2 / math.sqrt(volume), 1.0 / math.sqrt(orbitals),
+        ),
+        out_shape=jax.ShapeDtypeStruct((orbitals, orbitals), half_type),
+        in_specs=[pl.BlockSpec(memory_space=pltpu.VMEM)] * 4,
+        out_specs=pl.BlockSpec(memory_space=pltpu.VMEM),
+        scratch_shapes=[
+            pieces, pltpu.VMEM((volume, 2, size, size), jnp.float32), pieces, pieces,
+            whole, whole, whole, pieces, pieces, pieces,
+            block, block, block, wide, wide, pltpu.VMEM((orbitals, orbitals), jnp.float32),
+            pltpu.SemaphoreType.DMA((4, volume, 2)), pltpu.SemaphoreType.DMA((4, volume, 2)),
+            pltpu.SemaphoreType.DMA((2,)), pltpu.SemaphoreType.DMA((2,)),
+        ],
+        compiler_params=pltpu.CompilerParams(
+            collective_id=0, has_side_effects=True, vmem_limit_bytes=40 * 2 ** 20
+        ),
+    )(green_blocks[0, 0], coulomb[0], couple_cols[0], couple_vals[0])
+    return result[None, None]
+
+
+def fused_grid(mesh):
+    volume = mesh.shape["energy"]
+    grid = math.isqrt(2 * volume)
+    return grid if grid * grid == 2 * volume and grid % 2 == 0 else 0
+
+
+def on_any(grid, green_blocks, coulomb, couple_cols, couple_vals):
+    orbitals = green_blocks.shape[-1]
+    fits = (
+        grid > 0
+        and green_blocks.shape[:2] == (1, 1)
+        and orbitals % (128 * max(grid, 1)) == 0
+        and couple_cols.shape[1] * grid == orbitals
+        and lax.axis_size("slab") > 1
+    )
+    if fits:
+        return fused_on_device(grid, green_blocks, coulomb, couple_cols, couple_vals)
+    return on_device(green_blocks, coulomb, couple_cols, couple_vals)
+
+
 def solution(mesh):
     return jax.shard_map(
-        on_device,
+        functools.partial(on_any, fused_grid(mesh)),
         mesh=mesh,
         in_specs=(
             P("energy", "slab", None, None),

time: 134 us -> 64.1 us (0.48)
  Pallas kernels: 0 us -> 58.5 us
  blocking collectives: 35.7 us -> 0 us
  waiting for transfers between devices: 23.9 us -> 0 us
  local copies, waits for them, and re-layouts: 27.8 us -> 4.34 us
  starting transfers between devices: 22.6 us -> 0 us
  other arithmetic: 13.7 us -> 0 us
  matrix products: 8.85 us -> 0 us
    pallas_call x0 -> x1, Pallas kernels: none -> 58.5 us  [fused_on_device(): pl.pallas_call(functools.partial(fused_kernel, volume, slabs, grid, 0.5 /...]
    all_to_all x2 -> x0, blocking collectives: 35.7 us -> none  [the longest x1 18 us: on_device(): lax.all_to_all(polar_entries.reshape(entry_shape), 'energy', split_axis=0...]
    all_to_all x3 -> x0, waiting for transfers between devices: 23.9 us -> none  [the longest x1 9.3 us: on_device(): lax.all_to_all(flipped, 'energy', split_axis=1, concat_axis=0, tiled=True)]
    all_to_all x3 -> x0, starting transfers between devices: 15.2 us -> none  [the longest x1 7.28 us: on_device(): lax.all_to_all(own_green, 'energy', split_axis=1, concat_axis=0, tiled=True)]
    unnamed x3 -> x0, other arithmetic: 12.4 us -> none
    all_to_all x3 -> x0, local copies, waits for them, and re-layouts: 10.8 us -> none  [the longest x1 3.87 us: on_device(): lax.all_to_all(flipped, 'energy', split_axis=1, concat_axis=0, tiled=True)]
    dot_general x18 -> x0, matrix products: 8.85 us -> none  [the longest x12 5.21 us: plain_dot(): return jnp.dot(left, right, preferred_element_type=jnp.float32)]
    ppermute x3 -> x0, starting transfers between devices: 7.36 us -> none  [from_behind(): return lax.ppermute(x, axis, pairs)]
  transfers between devices with their start and end apart: 6 -> 0, of which waited for: 3 -> 0; matrix products, arithmetic and copies ran while one was open for 9% -> 0% of each run, Pallas kernels for 0% -> 0%
where the time goes in v1:
time: 64.1 us; the launch traced here: 62.9 us
  Pallas kernels  58.5 us (91%)
  local copies, waits for them, and re-layouts  4.34 us (7%)
    pallas_call x1, Pallas kernels, fused_on_device(): pl.pallas_call(functools.partial(fused_kernel, volume, slabs, grid, 0.5 /...  58.5 us
    unnamed x11, local copies, waits for them, and re-layouts  4.34 us

profile of v1, /device:TPU:0, one launch (start us, length us, event | category | flops | bytes accessed | tf_op | source)
XLA Modules:
  0.0 62.9 jit_solution(16782425438929470983)
XLA Ops:
  0.0 0.0 copy-start.3
  0.0 0.7 %copy-done.3 = bf16[1,128,8]{1,2,0:T(8,128)(2,1)S(1)} copy-done((bf16[1,128,8]{1,2,0:T(8,128)(2,1)S(1)}, bf16[1,128,8]{1,2,0:T(8,128)(2,1)}, u32[]{:S(2)}) %copy-start.3) | copy-done | bytes 2072
  0.7 0.0 copy-start.2
  0.7 0.1 copy.6
  0.8 0.6 copy-done.2
  1.4 0.1 copy.5
  1.5 0.0 copy-start
  1.5 1.0 %copy-done = bf16[1,1,512,512]{3,2,1,0:T(8,128)(2,1)S(1)} copy-done((bf16[1,1,512,512]{3,2,1,0:T(8,128)(2,1)S(1)}, bf16[1,1,512,512]{3,2,1,0:T(8,128)(2,1)}, u32[]{:S(2)}) %copy-start) | copy-done | bytes 524312
  2.5 0.0 copy-start.1
  2.5 1.0 %copy-done.1 = bf16[1,512,512]{2,1,0:T(8,128)(2,1)S(1)} copy-done((bf16[1,512,512]{2,1,0:T(8,128)(2,1)S(1)}, bf16[1,512,512]{2,1,0:T(8,128)(2,1)}, u32[]{:S(2)}) %copy-start.1) | copy-done | bytes 524312
  3.6 58.5 %shard_map.46 = bf16[512,512]{1,0:T(8,128)(2,1)S(1)} custom-call(bf16[512,512]{1,0:T(8,128)(2,1)S(1)} %bitcast.6, bf16[512,512]{1,0:T(8,128)(2,1)S(1)} %bitcast.7, s32[128,8]{1,0:T(8,128)S(1)} %bitcast.8, bf16[128,8]{1,0:T(8,128)(2,1)S(1)} %bitcast.9), custom_call_target="tpu_custom_call" | custom-call | tf_op jit(solution)/shard_map/pallas_call | solution.py:375
  62.1 0.8 %copy.8 = bf16[1,1,512,512]{3,2,1,0:T(8,128)(2,1)} copy(bf16[1,1,512,512]{3,2,1,0:T(8,128)(2,1)S(1)} %bitcast.5) | data formatting | bytes 1048576
Async XLA Ops:
  0.0 0.7 %copy-start.3 = (bf16[1,128,8]{1,2,0:T(8,128)(2,1)S(1)}, bf16[1,128,8]{1,2,0:T(8,128)(2,1)}, u32[]{:S(2)}) copy-start(bf16[1,128,8]{1,2,0:T(8,128)(2,1)} %param.7) | copy-start | bytes 6148
  0.7 0.7 %copy-start.2 = (s32[1,128,8]{1,2,0:T(8,128)S(1)}, s32[1,128,8]{1,2,0:T(8,128)}, u32[]{:S(2)}) copy-start(s32[1,128,8]{1,2,0:T(8,128)} %param.6) | copy-start | bytes 12292
  1.5 1.0 %copy-start = (bf16[1,1,512,512]{3,2,1,0:T(8,128)(2,1)S(1)}, bf16[1,1,512,512]{3,2,1,0:T(8,128)(2,1)}, u32[]{:S(2)}) copy-start(bf16[1,1,512,512]{3,2,1,0:T(8,128)(2,1)} %param.4) | copy-start | bytes 1572868
  2.5 1.0 %copy-start.1 = (bf16[1,512,512]{2,1,0:T(8,128)(2,1)S(1)}, bf16[1,512,512]{2,1,0:T(8,128)(2,1)}, u32[]{:S(2)}) copy-start(bf16[1,512,512]{2,1,0:T(8,128)(2,1)} %param.5) | copy-start | bytes 1572868

commit v2 on v1

--- a/solution.py
+++ b/solution.py
@@ -170,11 +170,20 @@
 
 def fused_kernel(
     volume, slabs, grid, scale_polar, scale_sigma, inv_root,
-    green, coulomb, cols, vals, out,
-    green_in, mirror, polar_out, polar_in, matrix, inner, screened, screen_in, sigma_out, sigma_in,
+    green_hbm, coulomb_hbm, cols_hbm, vals_hbm, out,
+    green, coulomb, cols, vals,
+    green_in, mirror, polar_out, polar_in, polar_more, matrix, inner, screened, screen_in, sigma_out, sigma_in,
     coupling, turned, next_corner, left_out, left_in, total,
-    send_sem, recv_sem, slab_send, slab_recv,
+    send_sem, recv_sem, wave_send, wave_recv, more_send, more_recv, slab_send, slab_recv, load_sem,
 ):
+    loads = [
+        pltpu.make_async_copy(source, target, load_sem.at[n])
+        for n, (source, target) in enumerate(
+            ((green_hbm, green), (coulomb_hbm, coulomb), (cols_hbm, cols), (vals_hbm, vals))
+        )
+    ]
+    for load in loads:
+        load.start()
     me = lax.axis_index("energy")
     slab = lax.axis_index("slab")
     size = green.shape[0] // grid
@@ -182,7 +191,13 @@
     order = sorted(range(1, volume), key=lambda k: (-min(k, volume - k), k))
     has_prev = 1 - (slabs - 1 - slab + 0) // (slabs - 1)
     has_next = 1 - slab // (slabs - 1)
-    diagonal = me // (grid * (grid - 1) // 2)
+    paired = grid * (grid - 1) // 2
+    diagonal = me // paired
+    pairs = volume // 2
+    side = lax.rem(slab, 2)
+    unit_here = me // 2
+    hosting = lax.rem(me, 2) == side
+    zero_unit = 1 - (unit_here + pairs - 1) // pairs
 
     def peer_of(k):
         return lax.rem(me + k, volume)
@@ -246,6 +261,7 @@
                 row, col = coords[half]
                 target[row * size:(row + 1) * size, col * size:(col + 1) * size] = landing[unit, half]
 
+    loads[0].wait()
     sent = scatter(green, green_in, 0)
     corner_copy = pltpu.make_async_remote_copy(
         src_ref=green.at[pl.ds(0, size), pl.ds(0, size)], dst_ref=next_corner,
@@ -262,6 +278,8 @@
     def _():
         corner_copy.start()
 
+    loads[2].wait()
+    loads[3].wait()
     ids = cols[...]
     values = vals[...].astype(jnp.float32)
     columns = lax.broadcasted_iota(jnp.int32, (size, size), 1)
@@ -291,12 +309,29 @@
 
         lax.fori_loop(0, volume, flip, 0)
 
+    def polar_copy(unit, half, piece):
+        return pltpu.make_async_remote_copy(
+            src_ref=piece, dst_ref=polar_in.at[me, half],
+            send_sem=send_sem.at[1, unit, half], recv_sem=recv_sem.at[1, me, half],
+            device_id=(2 * unit + side, slab), device_id_type=MESH,
+        )
+
+    def more_copy(half):
+        return pltpu.make_async_remote_copy(
+            src_ref=polar_out.at[half * pairs, 1], dst_ref=polar_more.at[me - paired, half],
+            send_sem=more_send.at[half], recv_sem=more_recv.at[me - paired, half],
+            device_id=(side, slab), device_id_type=MESH,
+        )
+
+    def polar_piece(unit, half):
+        return polar_out.at[unit, half] if unit > 0 else polar_out.at[half * pairs, 0]
+
     for half in range(2):
         def correlate(step, carry, half=half):
             rows = pl.ds(pl.multiple_of(step * rows_at_once, rows_at_once), rows_at_once)
             mine = [green_in[e, half, rows, :].astype(jnp.float32) for e in range(volume)]
             theirs = [mirror[e, half, rows, :] for e in range(volume)]
-            for e in range(volume):
+            for e in range(pairs + 1):
                 acc = mine[0] * theirs[(0 - e) % volume]
                 for e2 in range(1, volume):
                     acc += mine[e2] * theirs[(e2 - e) % volume]
@@ -304,26 +339,122 @@
             return carry
 
         lax.fori_loop(0, size // rows_at_once, correlate, 0)
-        copies = gather(polar_out, polar_in, 1, half)
-        everything += copies
-        if half == 0:
-            polar_copies = copies
-        else:
-            polar_copies = polar_copies + copies
-    arrived(polar_copies)
-    assemble(polar_in, matrix)
-    inner[...] = plain_dot(coulomb[...], matrix[...]).astype(jnp.bfloat16)
-    second = plain_dot(inner[...], coulomb[...])
-    total[...] = second
-    matrix[...] = second.astype(jnp.bfloat16)
-    third = plain_dot(inner[...], matrix[...])
-    screened[...] = (coulomb[...].astype(jnp.float32) + total[...] + third).astype(jnp.bfloat16)
-    copies = scatter(screened, screen_in, 2)
-    everything += copies
-    arrived(copies)
+        for unit in range(pairs):
+            ready = (half,) if unit > 0 else ((0, 1) if half == 0 else ())
+            for part in ready:
+                piece = polar_piece(unit, part)
+
+                @pl.when(me != 2 * unit + side)
+                def _(unit=unit, part=part, piece=piece):
+                    polar_copy(unit, part, piece).start()
+
+                @pl.when(me == 2 * unit + side)
+                def _(part=part, piece=piece):
+                    polar_in[me, part] = piece[...]
+
+        if half == 1:
+            @pl.when(me >= paired)
+            def _():
+                for part in range(2):
+                    more_copy(part).start()
+
+    other_energy = zero_unit * pairs + (1 - zero_unit) * (volume - unit_here)
+    energies_here = (unit_here, other_energy)
+
+    def wave_copy(which, k, half):
+        coords = unit_blocks(peer_of(k), grid)[half]
+        return pltpu.make_async_remote_copy(
+            src_ref=block_of(screened.at[which], coords), dst_ref=screen_in.at[energies_here[which], half],
+            send_sem=wave_send.at[which, k, half], recv_sem=wave_recv.at[energies_here[which], half],
+            device_id=(peer_of(k), slab), device_id_type=MESH,
+        )
+
+    def send_waves(which, half):
+        for k in order:
+            wave_copy(which, k, half).start()
+        own = unit_blocks(me, grid)[half]
+        screen_in[energies_here[which], half] = block_of(screened.at[which], own)[...]
+
+    def screen(which):
+        inner[...] = plain_dot(coulomb[...], matrix[which]).astype(jnp.bfloat16)
+        total[...] = plain_dot(inner[...], coulomb[...])
+        matrix[which] = total[...].astype(jnp.bfloat16)
+        third = plain_dot(inner[...], matrix[which])
+        screened[which] = (coulomb[...].astype(jnp.float32) + total[...] + third).astype(jnp.bfloat16)
+
+    def span(index):
+        return slice(index * size, (index + 1) * size)
+
+    def flipped(block):
+        return block.astype(jnp.float32).T.astype(jnp.bfloat16)
+
+    @pl.when(hosting)
+    def _():
+        for source in range(volume):
+            @pl.when(me != source)
+            def _(source=source):
+                for half in range(2):
+                    pltpu.make_async_remote_copy(
+                        src_ref=polar_out.at[0, half], dst_ref=polar_in.at[source, half],
+                        send_sem=send_sem.at[1, 0, half], recv_sem=recv_sem.at[1, source, half],
+                        device_id=(source, slab), device_id_type=MESH,
+                    ).wait_recv()
+
+        @pl.when(unit_here == 0)
+        def _():
+            for source in range(volume - paired):
+                for half in range(2):
+                    pltpu.make_async_remote_copy(
+                        src_ref=polar_out.at[0, half], dst_ref=polar_more.at[source, half],
+                        send_sem=more_send.at[half], recv_sem=more_recv.at[source, half],
+                        device_id=(source + paired, slab), device_id_type=MESH,
+                    ).wait_recv()
+            for which in range(2):
+                for unit in range(volume):
+                    (row0, col0), (row1, col1) = unit_blocks(unit, grid)
+                    block = polar_in[unit, which]
+                    matrix[which, span(row0), span(col0)] = block
+                    matrix[which, span(row1), span(col1)] = (
+                        flipped(block) if unit < paired else polar_more[unit - paired, which]
+                    )
+
+        @pl.when(unit_here > 0)
+        def _():
+            for unit in range(volume):
+                for half in range(2):
+                    row, col = unit_blocks(unit, grid)[half]
+                    block = polar_in[unit, half]
+                    matrix[0, span(row), span(col)] = block
+                    matrix[1, span(col), span(row)] = flipped(block)
+
+        loads[1].wait()
+        screen(0)
+        send_waves(0, 0)
+        screen(1)
+        send_waves(1, 0)
+        send_waves(0, 1)
+        send_waves(1, 1)
+
+    @pl.when(lax.rem(me, 2) != side)
+    def _():
+        loads[1].wait()
+
+    def waves_arrived(half):
+        for e in range(volume):
+            source = 2 * (0 if e == pairs else min(e, volume - e)) + side
+
+            @pl.when(me != source)
+            def _(e=e, source=source):
+                pltpu.make_async_remote_copy(
+                    src_ref=screen_in.at[e, half], dst_ref=screen_in.at[e, half],
+                    send_sem=wave_send.at[0, 0, half], recv_sem=wave_recv.at[e, half],
+                    device_id=(source, slab), device_id_type=MESH,
+                ).wait_recv()
 
     sigma_copies = []
     for half in range(2):
+        waves_arrived(half)
+
         def convolve(step, carry, half=half):
             rows = pl.ds(pl.multiple_of(step * rows_at_once, rows_at_once), rows_at_once)
             mine = [green_in[e, half, rows, :].astype(jnp.float32) for e in range(volume)]
@@ -339,27 +470,45 @@
         sigma_copies += gather(sigma_out, sigma_in, 3, half)
     everything += sigma_copies
     arrived(sigma_copies)
-    assemble(sigma_in, matrix)
+    plane = matrix.at[0]
+    assemble(sigma_in, plane)
 
     @pl.when(slab < slabs - 1)
     def _():
         corner_copy.wait_recv()
         near_next = plain_dot(coupling[...], next_corner[...]).astype(jnp.bfloat16)
         right_part = plain_dot(near_next, turned[...]) * inv_root
-        matrix[last:, last:] = (matrix[last:, last:].astype(jnp.float32) + right_part).astype(jnp.bfloat16)
+        plane[last:, last:] = (plane[last:, last:].astype(jnp.float32) + right_part).astype(jnp.bfloat16)
         left_copy.wait_send()
 
     @pl.when(slab > 0)
     def _():
         left_copy.wait_recv()
-        matrix[:size, :size] = (matrix[:size, :size].astype(jnp.float32) + left_in[...]).astype(jnp.bfloat16)
+        plane[:size, :size] = (plane[:size, :size].astype(jnp.float32) + left_in[...]).astype(jnp.bfloat16)
         corner_copy.wait_send()
 
-    inner[...] = plain_dot(green[...], matrix[...]).astype(jnp.bfloat16)
+    inner[...] = plain_dot(green[...], plane[...]).astype(jnp.bfloat16)
     updated = green[...].astype(jnp.float32) + plain_dot(inner[...], green[...]) * inv_root
     out[...] = updated.astype(jnp.bfloat16)
     for copy in everything:
         copy.wait_send()
+    for unit in range(pairs):
+        @pl.when(me != 2 * unit + side)
+        def _(unit=unit):
+            for half in range(2):
+                polar_copy(unit, half, polar_piece(unit, half)).wait_send()
+
+    @pl.when(me >= paired)
+    def _():
+        for half in range(2):
+            more_copy(half).wait_send()
+
+    @pl.when(hosting)
+    def _():
+        for half in range(2):
+            for which in range(2):
+                for k in order:
+                    wave_copy(which, k, half).wait_send()
 
 
 def fused_on_device(grid, green_blocks, coulomb, couple_cols, couple_vals):
@@ -370,6 +519,7 @@
     half_type = jnp.bfloat16
     pieces = pltpu.VMEM((volume, 2, size, size), half_type)
     whole = pltpu.VMEM((orbitals, orbitals), half_type)
+    two = pltpu.VMEM((2, orbitals, orbitals), half_type)
     block = pltpu.VMEM((size, size), half_type)
     wide = pltpu.VMEM((size, size), jnp.float32)
     result = pl.pallas_call(
@@ -378,14 +528,18 @@
             0.5 / math.sqrt(orbitals * volume), 0.2 / math.sqrt(volume), 1.0 / math.sqrt(orbitals),
         ),
         out_shape=jax.ShapeDtypeStruct((orbitals, orbitals), half_type),
-        in_specs=[pl.BlockSpec(memory_space=pltpu.VMEM)] * 4,
+        in_specs=[pl.BlockSpec(memory_space=pltpu.HBM)] * 4,
         out_specs=pl.BlockSpec(memory_space=pltpu.VMEM),
         scratch_shapes=[
+            whole, whole, pltpu.VMEM(couple_cols.shape[1:], jnp.int32), pltpu.VMEM(couple_vals.shape[1:], half_type),
             pieces, pltpu.VMEM((volume, 2, size, size), jnp.float32), pieces, pieces,
-            whole, whole, whole, pieces, pieces, pieces,
+            pltpu.VMEM((grid // 2, 2, size, size), half_type),
+            two, whole, two, pieces, pieces, pieces,
             block, block, block, wide, wide, pltpu.VMEM((orbitals, orbitals), jnp.float32),
             pltpu.SemaphoreType.DMA((4, volume, 2)), pltpu.SemaphoreType.DMA((4, volume, 2)),
-            pltpu.SemaphoreType.DMA((2,)), pltpu.SemaphoreType.DMA((2,)),
+            pltpu.SemaphoreType.DMA((2, volume, 2)), pltpu.SemaphoreType.DMA((volume, 2)),
+            pltpu.SemaphoreType.DMA((2,)), pltpu.SemaphoreType.DMA((grid // 2, 2)),
+            pltpu.SemaphoreType.DMA((2,)), pltpu.SemaphoreType.DMA((2,)), pltpu.SemaphoreType.DMA((4,)),
         ],
         compiler_params=pltpu.CompilerParams(
             collective_id=0, has_side_effects=True, vmem_limit_bytes=40 * 2 ** 20

time: 64.1 us -> 64.8 us (1.011); the launches traced: 62.9 us -> 64.5 us
  Pallas kernels: 58.5 us -> 60.2 us
    pallas_call x1, Pallas kernels: 58.5 us -> 60.2 us  [fused_on_device(): pl.pallas_call(functools.partial(fused_kernel, volume, slabs, grid, 0.5 /...]
where the time goes in v2:
time: 64.8 us; the launch traced here: 64.5 us
  Pallas kernels  60.2 us (93%)
  local copies, waits for them, and re-layouts  4.34 us (7%)
    pallas_call x1, Pallas kernels, fused_on_device(): pl.pallas_call(functools.partial(fused_kernel, volume, slabs, grid, 0.5 /...  60.2 us
    unnamed x11, local copies, waits for them, and re-layouts  4.34 us

profile of v2, /device:TPU:0, one launch (start us, length us, event | category | flops | bytes accessed | tf_op | source)
XLA Modules:
  0.0 64.5 jit_solution(17871063164646771917)
XLA Ops:
  0.0 0.0 copy-start.3
  0.0 0.7 %copy-done.3 = bf16[1,128,8]{1,2,0:T(8,128)(2,1)S(1)} copy-done((bf16[1,128,8]{1,2,0:T(8,128)(2,1)S(1)}, bf16[1,128,8]{1,2,0:T(8,128)(2,1)}, u32[]{:S(2)}) %copy-start.3) | copy-done | bytes 2072
  0.7 0.0 copy-start.2
  0.7 0.1 copy.6
  0.8 0.6 copy-done.2
  1.4 0.1 copy.5
  1.5 0.0 copy-start
  1.5 1.0 %copy-done = bf16[1,1,512,512]{3,2,1,0:T(8,128)(2,1)S(1)} copy-done((bf16[1,1,512,512]{3,2,1,0:T(8,128)(2,1)S(1)}, bf16[1,1,512,512]{3,2,1,0:T(8,128)(2,1)}, u32[]{:S(2)}) %copy-start) | copy-done | bytes 524312
  2.5 0.0 copy-start.1
  2.5 1.0 %copy-done.1 = bf16[1,512,512]{2,1,0:T(8,128)(2,1)S(1)} copy-done((bf16[1,512,512]{2,1,0:T(8,128)(2,1)S(1)}, bf16[1,512,512]{2,1,0:T(8,128)(2,1)}, u32[]{:S(2)}) %copy-start.1) | copy-done | bytes 524312
  3.6 60.2 %shard_map.46 = bf16[512,512]{1,0:T(8,128)(2,1)S(1)} custom-call(bf16[512,512]{1,0:T(8,128)(2,1)S(1)} %bitcast.6, bf16[512,512]{1,0:T(8,128)(2,1)S(1)} %bitcast.7, s32[128,8]{1,0:T(8,128)S(1)} %bitcast.8, bf16[128,8]{1,0:T(8,128)(2,1)S(1)} %bitcast.9), custom_call_target="tpu_custom_call" | custom-call | tf_op jit(solution)/shard_map/pallas_call | solution.py:525
  63.7 0.8 %copy.8 = bf16[1,1,512,512]{3,2,1,0:T(8,128)(2,1)} copy(bf16[1,1,512,512]{3,2,1,0:T(8,128)(2,1)S(1)} %bitcast.5) | data formatting | bytes 1048576
Async XLA Ops:
  0.0 0.7 %copy-start.3 = (bf16[1,128,8]{1,2,0:T(8,128)(2,1)S(1)}, bf16[1,128,8]{1,2,0:T(8,128)(2,1)}, u32[]{:S(2)}) copy-start(bf16[1,128,8]{1,2,0:T(8,128)(2,1)} %param.7) | copy-start | bytes 6148
  0.7 0.7 %copy-start.2 = (s32[1,128,8]{1,2,0:T(8,128)S(1)}, s32[1,128,8]{1,2,0:T(8,128)}, u32[]{:S(2)}) copy-start(s32[1,128,8]{1,2,0:T(8,128)} %param.6) | copy-start | bytes 12292
  1.5 1.0 %copy-start = (bf16[1,1,512,512]{3,2,1,0:T(8,128)(2,1)S(1)}, bf16[1,1,512,512]{3,2,1,0:T(8,128)(2,1)}, u32[]{:S(2)}) copy-start(bf16[1,1,512,512]{3,2,1,0:T(8,128)(2,1)} %param.4) | copy-start | bytes 1572868
  2.5 1.0 %copy-start.1 = (bf16[1,512,512]{2,1,0:T(8,128)(2,1)S(1)}, bf16[1,512,512]{2,1,0:T(8,128)(2,1)}, u32[]{:S(2)}) copy-start(bf16[1,512,512]{2,1,0:T(8,128)(2,1)} %param.5) | copy-start | bytes 1572868

commit v3 on v1

--- a/solution.py
+++ b/solution.py
@@ -170,11 +170,20 @@
 
 def fused_kernel(
     volume, slabs, grid, scale_polar, scale_sigma, inv_root,
-    green, coulomb, cols, vals, out,
+    green_hbm, coulomb_hbm, cols_hbm, vals_hbm, out,
+    green, coulomb, cols, vals,
     green_in, mirror, polar_out, polar_in, matrix, inner, screened, screen_in, sigma_out, sigma_in,
-    coupling, turned, next_corner, left_out, left_in, total,
-    send_sem, recv_sem, slab_send, slab_recv,
+    coupling, turned, next_corner, left_out, left_in, right_in, total,
+    send_sem, recv_sem, slab_send, slab_recv, load_sem,
 ):
+    loads = [
+        pltpu.make_async_copy(source, target, load_sem.at[n])
+        for n, (source, target) in enumerate(
+            ((green_hbm, green), (coulomb_hbm, coulomb), (cols_hbm, cols), (vals_hbm, vals))
+        )
+    ]
+    for load in loads:
+        load.start()
     me = lax.axis_index("energy")
     slab = lax.axis_index("slab")
     size = green.shape[0] // grid
@@ -215,9 +224,9 @@
 
     def scatter(source, landing, phase):
         copies = []
-        for k in order:
-            coords = unit_blocks(peer_of(k), grid)
-            for half in range(2):
+        for half in range(2):
+            for k in order:
+                coords = unit_blocks(peer_of(k), grid)
                 copy = remote(block_of(source, coords[half]), landing.at[me, half], phase, k, half)
                 copy.start()
                 copies.append(copy)
@@ -239,13 +248,19 @@
         for copy in copies:
             copy.wait_recv()
 
-    def assemble(landing, target):
-        for unit in range(volume):
-            coords = unit_blocks(unit, grid)
-            for half in range(2):
-                row, col = coords[half]
-                target[row * size:(row + 1) * size, col * size:(col + 1) * size] = landing[unit, half]
-
+    def from_of(k):
+        return lax.rem(me + volume - k, volume)
+
+    def place(landing, target, source, half):
+        block_of(target, unit_blocks(source, grid)[half])[...] = landing[source, half]
+
+    def assemble(landing, target, copies, half):
+        place(landing, target, me, half)
+        for k, copy in zip(order, copies):
+            copy.wait_recv()
+            place(landing, target, from_of(k), half)
+
+    loads[0].wait()
     sent = scatter(green, green_in, 0)
     corner_copy = pltpu.make_async_remote_copy(
         src_ref=green.at[pl.ds(0, size), pl.ds(0, size)], dst_ref=next_corner,
@@ -262,6 +277,8 @@
     def _():
         corner_copy.start()
 
+    loads[2].wait()
+    loads[3].wait()
     ids = cols[...]
     values = vals[...].astype(jnp.float32)
     columns = lax.broadcasted_iota(jnp.int32, (size, size), 1)
@@ -278,19 +295,20 @@
         left_out[...] = plain_dot(near_prev, coupling[...]) * inv_root
         left_copy.start()
 
-    arrived(sent)
     everything = list(sent)
     rows_at_once = 16
 
+    def flip(e, half):
+        to = diagonal * half + (1 - diagonal) * (1 - half)
+        mirror[e, to] = green_in[e, half].astype(jnp.float32).T
+
     for half in range(2):
-        other = diagonal * half + (1 - diagonal) * (1 - half)
-
-        def flip(e, carry, half=half, other=other):
-            mirror[e, half] = green_in[e, other].astype(jnp.float32).T
-            return carry
-
-        lax.fori_loop(0, volume, flip, 0)
-
+        flip(me, half)
+        for k, copy in zip(order, sent[half * len(order):]):
+            copy.wait_recv()
+            flip(from_of(k), half)
+
+    polar_copies = []
     for half in range(2):
         def correlate(step, carry, half=half):
             rows = pl.ds(pl.multiple_of(step * rows_at_once, rows_at_once), rows_at_once)
@@ -306,12 +324,10 @@
         lax.fori_loop(0, size // rows_at_once, correlate, 0)
         copies = gather(polar_out, polar_in, 1, half)
         everything += copies
-        if half == 0:
-            polar_copies = copies
-        else:
-            polar_copies = polar_copies + copies
-    arrived(polar_copies)
-    assemble(polar_in, matrix)
+        polar_copies.append(copies)
+    loads[1].wait()
+    for half in range(2):
+        assemble(polar_in, matrix, polar_copies[half], half)
     inner[...] = plain_dot(coulomb[...], matrix[...]).astype(jnp.bfloat16)
     second = plain_dot(inner[...], coulomb[...])
     total[...] = second
@@ -320,10 +336,12 @@
     screened[...] = (coulomb[...].astype(jnp.float32) + total[...] + third).astype(jnp.bfloat16)
     copies = scatter(screened, screen_in, 2)
     everything += copies
-    arrived(copies)
+    waves = copies
 
     sigma_copies = []
     for half in range(2):
+        arrived(waves[half * len(order):(half + 1) * len(order)])
+
         def convolve(step, carry, half=half):
             rows = pl.ds(pl.multiple_of(step * rows_at_once, rows_at_once), rows_at_once)
             mine = [green_in[e, half, rows, :].astype(jnp.float32) for e in range(volume)]
@@ -336,17 +354,22 @@
             return carry
 
         lax.fori_loop(0, size // rows_at_once, convolve, 0)
-        sigma_copies += gather(sigma_out, sigma_in, 3, half)
-    everything += sigma_copies
-    arrived(sigma_copies)
-    assemble(sigma_in, matrix)
+        copies = gather(sigma_out, sigma_in, 3, half)
+        everything += copies
+        sigma_copies.append(copies)
 
     @pl.when(slab < slabs - 1)
     def _():
         corner_copy.wait_recv()
         near_next = plain_dot(coupling[...], next_corner[...]).astype(jnp.bfloat16)
-        right_part = plain_dot(near_next, turned[...]) * inv_root
-        matrix[last:, last:] = (matrix[last:, last:].astype(jnp.float32) + right_part).astype(jnp.bfloat16)
+        right_in[...] = plain_dot(near_next, turned[...]) * inv_root
+
+    for half in range(2):
+        assemble(sigma_in, matrix, sigma_copies[half], half)
+
+    @pl.when(slab < slabs - 1)
+    def _():
+        matrix[last:, last:] = (matrix[last:, last:].astype(jnp.float32) + right_in[...]).astype(jnp.bfloat16)
         left_copy.wait_send()
 
     @pl.when(slab > 0)
@@ -378,14 +401,15 @@
             0.5 / math.sqrt(orbitals * volume), 0.2 / math.sqrt(volume), 1.0 / math.sqrt(orbitals),
         ),
         out_shape=jax.ShapeDtypeStruct((orbitals, orbitals), half_type),
-        in_specs=[pl.BlockSpec(memory_space=pltpu.VMEM)] * 4,
+        in_specs=[pl.BlockSpec(memory_space=pltpu.HBM)] * 4,
         out_specs=pl.BlockSpec(memory_space=pltpu.VMEM),
         scratch_shapes=[
+            whole, whole, pltpu.VMEM(couple_cols.shape[1:], jnp.int32), pltpu.VMEM(couple_vals.shape[1:], half_type),
             pieces, pltpu.VMEM((volume, 2, size, size), jnp.float32), pieces, pieces,
             whole, whole, whole, pieces, pieces, pieces,
-            block, block, block, wide, wide, pltpu.VMEM((orbitals, orbitals), jnp.float32),
+            block, block, block, wide, wide, wide, pltpu.VMEM((orbitals, orbitals), jnp.float32),
             pltpu.SemaphoreType.DMA((4, volume, 2)), pltpu.SemaphoreType.DMA((4, volume, 2)),
-            pltpu.SemaphoreType.DMA((2,)), pltpu.SemaphoreType.DMA((2,)),
+            pltpu.SemaphoreType.DMA((2,)), pltpu.SemaphoreType.DMA((2,)), pltpu.SemaphoreType.DMA((4,)),
         ],
         compiler_params=pltpu.CompilerParams(
             collective_id=0, has_side_effects=True, vmem_limit_bytes=40 * 2 ** 20

time: 64.1 us -> 62.7 us (0.978)
  Pallas kernels: 58.5 us -> 57.5 us
    pallas_call x1, Pallas kernels: 58.5 us -> 57.5 us  [fused_on_device(): pl.pallas_call(functools.partial(fused_kernel, volume, slabs, grid, 0.5 /...]
where the time goes in v3:
time: 62.7 us; the launch traced here: 61.8 us
  Pallas kernels  57.5 us (92%)
  local copies, waits for them, and re-layouts  4.34 us (7%)
    pallas_call x1, Pallas kernels, fused_on_device(): pl.pallas_call(functools.partial(fused_kernel, volume, slabs, grid, 0.5 /...  57.5 us
    unnamed x11, local copies, waits for them, and re-layouts  4.34 us

profile of v3, /device:TPU:0, one launch (start us, length us, event | category | flops | bytes accessed | tf_op | source)
XLA Modules:
  0.0 61.8 jit_solution(10315429593539958133)
XLA Ops:
  0.0 0.0 copy-start.3
  0.0 0.7 %copy-done.3 = bf16[1,128,8]{1,2,0:T(8,128)(2,1)S(1)} copy-done((bf16[1,128,8]{1,2,0:T(8,128)(2,1)S(1)}, bf16[1,128,8]{1,2,0:T(8,128)(2,1)}, u32[]{:S(2)}) %copy-start.3) | copy-done | bytes 2072
  0.7 0.0 copy-start.2
  0.7 0.1 copy.6
  0.8 0.6 copy-done.2
  1.4 0.1 copy.5
  1.5 0.0 copy-start
  1.5 1.0 %copy-done = bf16[1,1,512,512]{3,2,1,0:T(8,128)(2,1)S(1)} copy-done((bf16[1,1,512,512]{3,2,1,0:T(8,128)(2,1)S(1)}, bf16[1,1,512,512]{3,2,1,0:T(8,128)(2,1)}, u32[]{:S(2)}) %copy-start) | copy-done | bytes 524312
  2.5 0.0 copy-start.1
  2.5 1.0 %copy-done.1 = bf16[1,512,512]{2,1,0:T(8,128)(2,1)S(1)} copy-done((bf16[1,512,512]{2,1,0:T(8,128)(2,1)S(1)}, bf16[1,512,512]{2,1,0:T(8,128)(2,1)}, u32[]{:S(2)}) %copy-start.1) | copy-done | bytes 524312
  3.6 57.5 %shard_map.46 = bf16[512,512]{1,0:T(8,128)(2,1)S(1)} custom-call(bf16[512,512]{1,0:T(8,128)(2,1)S(1)} %bitcast.6, bf16[512,512]{1,0:T(8,128)(2,1)S(1)} %bitcast.7, s32[128,8]{1,0:T(8,128)S(1)} %bitcast.8, bf16[128,8]{1,0:T(8,128)(2,1)S(1)} %bitcast.9), custom_call_target="tpu_custom_call" | custom-call | tf_op jit(solution)/shard_map/pallas_call | solution.py:398
  61.1 0.8 %copy.8 = bf16[1,1,512,512]{3,2,1,0:T(8,128)(2,1)} copy(bf16[1,1,512,512]{3,2,1,0:T(8,128)(2,1)S(1)} %bitcast.5) | data formatting | bytes 1048576
Async XLA Ops:
  0.0 0.7 %copy-start.3 = (bf16[1,128,8]{1,2,0:T(8,128)(2,1)S(1)}, bf16[1,128,8]{1,2,0:T(8,128)(2,1)}, u32[]{:S(2)}) copy-start(bf16[1,128,8]{1,2,0:T(8,128)(2,1)} %param.7) | copy-start | bytes 6148
  0.7 0.7 %copy-start.2 = (s32[1,128,8]{1,2,0:T(8,128)S(1)}, s32[1,128,8]{1,2,0:T(8,128)}, u32[]{:S(2)}) copy-start(s32[1,128,8]{1,2,0:T(8,128)} %param.6) | copy-start | bytes 12292
  1.5 1.0 %copy-start = (bf16[1,1,512,512]{3,2,1,0:T(8,128)(2,1)S(1)}, bf16[1,1,512,512]{3,2,1,0:T(8,128)(2,1)}, u32[]{:S(2)}) copy-start(bf16[1,1,512,512]{3,2,1,0:T(8,128)(2,1)} %param.4) | copy-start | bytes 1572868
  2.5 1.0 %copy-start.1 = (bf16[1,512,512]{2,1,0:T(8,128)(2,1)S(1)}, bf16[1,512,512]{2,1,0:T(8,128)(2,1)}, u32[]{:S(2)}) copy-start(bf16[1,512,512]{2,1,0:T(8,128)(2,1)} %param.5) | copy-start | bytes 1572868
